TPU v7x, 32 devices: a whole 2x2x4 slice. The times are simulated.
32 devices in a mesh: dp: 4 (over z), ep: 8 (over y, x, core).
Axes of the slice: x: 2, y: 2, z: 4, core: 2. Of those that a mesh axis runs over, the one named last changes fastest.
Arguments:
- x_norm: bfloat16 [8192, 4096], P(('dp', 'ep'))
- route_idx: int32 [8192, 2], P(('dp', 'ep'))
- w_router: bfloat16 [4096, 8], replicated
- w_gate: bfloat16 [8, 4096, 1376], P('ep')
- w_up: bfloat16 [8, 4096, 1376], P('ep')
- w_down: bfloat16 [8, 1376, 4096], P('ep')
- grad_out: bfloat16 [8192, 4096], P(('dp', 'ep'))
Outputs:
- output 1: bfloat16 [8192, 4096], P(('dp', 'ep'))
- output 2: float32 [8, 4096, 1376], P('ep')
- output 3: float32 [8, 4096, 1376], P('ep')
- output 4: float32 [8, 1376, 4096], P('ep')
- output 5: float32 [4096, 8], replicated
All inputs are finite; a program needn't handle non-finite values.
Results may differ from a plain program's by a relative error of at most 0.00526722.
Values are sent between devices in bfloat16 or wider.
A program may use at most 1 GiB of HBM per device.

v0:
```python
import jax
import jax.numpy as jnp
from jax import lax
from jax.sharding import PartitionSpec as P


def excl_cumsum(values, along_axis=0):
    return jnp.cumsum(values, axis=along_axis) - values


def segment_map(positions, from_start, to_start, seg_ends, total_rows):
    seg_index = jnp.sum(positions[:, None] >= seg_ends[None, :], axis=1)
    seg_index = jnp.minimum(seg_index, seg_ends.shape[0] - 1)
    mapped_pos = to_start[seg_index] + positions - from_start[seg_index]
    return jnp.where(positions < total_rows, mapped_pos, positions)


def rows_by_weight_t(left_rows, weights, group_sizes):
    dim_numbers = lax.RaggedDotDimensionNumbers(dot_dimension_numbers=(([1], [2]), ([], [])), lhs_ragged_dimensions=[0], rhs_group_dimensions=[0])
    return lax.ragged_dot_general(left_rows, weights, group_sizes, ragged_dot_dimension_numbers=dim_numbers, preferred_element_type=jnp.float32)


def group_outer(left_rows, right_rows, group_sizes):
    dim_numbers = lax.RaggedDotDimensionNumbers(dot_dimension_numbers=(([0], [0]), ([], [])), lhs_ragged_dimensions=[0], rhs_group_dimensions=[])
    return lax.ragged_dot_general(left_rows, right_rows, group_sizes, ragged_dot_dimension_numbers=dim_numbers, preferred_element_type=jnp.float32)


def expert_backward(x_rows, dy_rows, gate_rows, w_gate, w_up, w_down, group_sizes):
    z_gate = lax.ragged_dot(x_rows, w_gate, group_sizes, preferred_element_type=jnp.float32)
    z_up = lax.ragged_dot(x_rows, w_up, group_sizes, preferred_element_type=jnp.float32)
    sigmoid_z = jax.nn.sigmoid(z_gate)
    silu_z = z_gate * sigmoid_z
    act_rows = (silu_z * z_up).astype(jnp.bfloat16)
    out_rows = lax.ragged_dot(act_rows, w_down, group_sizes, preferred_element_type=jnp.float32)
    dy_wide = dy_rows.astype(jnp.float32)
    dgate_rows = jnp.sum(out_rows * dy_wide, axis=1)
    d_out = (gate_rows[:, None] * dy_wide).astype(jnp.bfloat16)
    d_act = rows_by_weight_t(d_out, w_down, group_sizes)
    d_zgate = (d_act * z_up * sigmoid_z * (1.0 + z_gate * (1.0 - sigmoid_z))).astype(jnp.bfloat16)
    d_zup = (d_act * silu_z).astype(jnp.bfloat16)
    dx_rows = (rows_by_weight_t(d_zgate, w_gate, group_sizes) + rows_by_weight_t(d_zup, w_up, group_sizes)).astype(jnp.bfloat16)
    grad_gate = group_outer(x_rows, d_zgate, group_sizes)
    grad_up = group_outer(x_rows, d_zup, group_sizes)
    grad_down = group_outer(act_rows, d_out, group_sizes)
    return dx_rows, dgate_rows, grad_gate, grad_up, grad_down


def router_backward(x_rows, route_idx, w_router, gate_probs, dgate):
    n_experts = w_router.shape[1]
    d_sel = gate_probs * (dgate - jnp.sum(gate_probs * dgate, axis=1, keepdims=True))
    expert_ids = jnp.arange(n_experts, dtype=jnp.int32)
    d_logits = jnp.sum(jnp.where(route_idx[:, :, None] == expert_ids, d_sel[:, :, None], 0.0), axis=1).astype(jnp.bfloat16)
    du_router = lax.dot_general(d_logits, w_router, (((1,), (1,)), ((), ())), preferred_element_type=jnp.float32)
    grad_router = lax.dot_general(x_rows, d_logits, (((0,), (0,)), ((), ())), preferred_element_type=jnp.float32)
    return du_router, grad_router


def solution(mesh):
    ep_size = mesh.shape["ep"]
    tok_spec = P(("dp", "ep"), None)
    exp_spec = P("ep", None, None)

    def device_step(x_loc, route_idx, w_router, w_gate, w_up, w_down, dy_loc):
        tok_dev, top_k = route_idx.shape
        model_dim = x_loc.shape[1]
        n_experts = w_router.shape[1]
        e_loc = w_gate.shape[0]
        n_choice = tok_dev * top_k
        capacity = 3 * tok_dev * top_k // n_experts
        other_max = (n_choice - capacity + n_experts - 2) // (n_experts - 1)
        send_max = min(capacity + (e_loc - 1) * other_max, tok_dev * min(top_k, e_loc))
        buf_rows = ep_size * send_max
        my_rank = lax.axis_index("ep")

        logits = jnp.dot(x_loc, w_router, preferred_element_type=jnp.float32)
        gate_probs = jax.nn.softmax(jnp.take_along_axis(logits, route_idx, axis=1), axis=-1)

        flat_exp = route_idx.reshape(n_choice)
        one_hot = (flat_exp[:, None] == jnp.arange(n_experts, dtype=jnp.int32)[None, :]).astype(jnp.int32)
        exp_count = jnp.sum(one_hot, axis=0)
        rank_in = jnp.sum((jnp.cumsum(one_hot, axis=0) - one_hot) * one_hot, axis=1)
        sorted_pos = excl_cumsum(exp_count)[flat_exp] + rank_in
        sorted_src = jnp.zeros((n_choice,), jnp.int32).at[sorted_pos].set(jnp.arange(n_choice, dtype=jnp.int32))
        owner_count = jnp.sum(exp_count.reshape(ep_size, e_loc), axis=1)
        send_offsets = excl_cumsum(owner_count)
        slot_i = jnp.arange(send_max, dtype=jnp.int32)
        block_pos = send_offsets[:, None] + slot_i[None, :]
        block_valid = (slot_i[None, :] < owner_count[:, None]).reshape(buf_rows)
        block_src = sorted_src[jnp.minimum(block_pos, n_choice - 1)].reshape(buf_rows)
        x_send = jnp.where(block_valid[:, None], x_loc[block_src // top_k], 0.0)
        dy_send = jnp.where(block_valid[:, None], dy_loc[block_src // top_k], 0.0)
        gate_send = jnp.where(block_valid, gate_probs.reshape(n_choice)[block_src], 0.0)

        count_all = lax.all_gather(exp_count, "ep")
        x_recv = lax.all_to_all(x_send, "ep", 0, 0, tiled=True)
        dy_recv = lax.all_to_all(dy_send, "ep", 0, 0, tiled=True)
        gate_recv = lax.all_to_all(gate_send, "ep", 0, 0, tiled=True)

        my_counts = lax.dynamic_slice_in_dim(count_all, my_rank * e_loc, e_loc, axis=1)
        group_sizes = jnp.sum(my_counts, axis=0)
        total_recv = jnp.sum(group_sizes)
        inner_start = excl_cumsum(my_counts, along_axis=1)
        blk_start = inner_start + jnp.arange(ep_size, dtype=jnp.int32)[:, None] * send_max
        exp_start = excl_cumsum(my_counts.T.reshape(-1)).reshape(e_loc, ep_size)
        positions = jnp.arange(buf_rows, dtype=jnp.int32)
        gather_pos = segment_map(positions, exp_start.reshape(-1), blk_start.T.reshape(-1), (exp_start + my_counts.T).reshape(-1), total_recv)
        local_exp = jnp.minimum(jnp.sum(slot_i[None, :, None] >= (inner_start + my_counts)[:, None, :], axis=2), e_loc - 1)
        start_sel = jnp.take_along_axis(exp_start.T, local_exp, axis=1)
        inner_sel = jnp.take_along_axis(inner_start, local_exp, axis=1)
        return_pos = jnp.clip(start_sel + slot_i[None, :] - inner_sel, 0, buf_rows - 1).reshape(buf_rows)

        dx_rows, dgate_rows, grad_gate, grad_up, grad_down = expert_backward(x_recv[gather_pos], dy_recv[gather_pos], gate_recv[gather_pos], w_gate, w_up, w_down, group_sizes)
        grad_gate = lax.psum(grad_gate, "dp")
        grad_up = lax.psum(grad_up, "dp")
        grad_down = lax.psum(grad_down, "dp")

        dx_back = lax.all_to_all(dx_rows[return_pos], "ep", 0, 0, tiled=True)
        dgate_back = lax.all_to_all(dgate_rows[return_pos], "ep", 0, 0, tiled=True)
        owner_of = flat_exp // e_loc
        back_idx = owner_of * send_max + sorted_pos - send_offsets[owner_of]
        dx_choice = dx_back[back_idx].reshape(tok_dev, top_k, model_dim)
        dgate = dgate_back[back_idx].reshape(tok_dev, top_k)
        du_router, grad_router = router_backward(x_loc, route_idx, w_router, gate_probs, dgate)
        grad_x = (jnp.sum(dx_choice.astype(jnp.float32), axis=1) + du_router).astype(jnp.bfloat16)
        grad_router = lax.psum(grad_router, ("dp", "ep"))
        return grad_x, grad_gate, grad_up, grad_down, grad_router

    return jax.shard_map(device_step, mesh=mesh, in_specs=(tok_spec, tok_spec, P(), exp_spec, exp_spec, exp_spec, tok_spec), out_specs=(tok_spec, exp_spec, exp_spec, exp_spec, P()), check_vma=False)
```

profile of v0, /device:TPU:0, one launch (start us, length us, event | category | flops | bytes accessed | tf_op | source)
XLA Modules:
  0.0 3210.1 jit_solution(6642076226901788269)
XLA Ops:
  29.6 23.9 gather_fusion.3
  63.0 13.4 broadcast_select_fusion.1
  76.5 143.9 %all_to_all.52 = bf16[8,192,4096]{2,1,0:T(8,128)(2,1)} all-to-all(bf16[8,192,4096]{2,1,0:T(8,128)(2,1)S(1)} %get-tuple-element.84), channel_id=1, replica_groups=mesh['dp'=4,'ep'=8] {'ep'}, dimensions={0} | all-to-all | bytes 25165824 | tf_op jit(solution)/shard_map/all_to_all | solution.py:96
  227.5 139.6 %all-reduce.1 = s32[8,8]{1,0:T(8,128)S(1)} all-reduce(s32[8,8]{1,0:T(8,128)S(1)} %reshape.737), channel_id=2, replica_groups=mesh['dp'=4,'ep'=8] {'ep'}, use_global_device_ids=true, to_apply=%add | all-reduce | flops 64 | bytes 512
  369.1 15.1 copy.59
  384.2 15.0 copy.60
  430.0 28.3 gather_fusion.4
  458.3 28.5 gather_fusion.6
  486.7 14.9 ragged-dot-none.7
  501.6 14.8 ragged-dot-none.6
  525.6 15.7 ragged-dot-none.3
  541.3 12.6 fusion.1
  563.0 41.7 %all-to-all-start.4 = ((f32[8,192,1]{1,2,0:T(1,128)}), f32[8,192,1]{1,2,0:T(1,128)S(1)}, u32[]{:S(2)}, u32[]{:S(2)}) async-start(f32[8,192,1]{1,2,0:T(1,128)} %all_to_all.46), calls=%async_computation.4 | async-start | bytes 16384 | tf_op jit(solution)/shard_map/all_to_all | solution.py:118
  627.2 15.3 copy.58
  663.6 14.8 ragged-dot-none.8
  678.4 13.7 multiply_convert_fusion.1
  692.1 20.5 ragged-dot-none
  712.7 21.5 ragged-dot-none.2
  734.2 21.2 ragged-dot-none.1
  755.5 15.2 ragged-dot-none.5
  770.7 15.2 ragged-dot-none.4
  785.9 21.2 add_convert_fusion
  807.1 28.3 gather_fusion.7
  835.4 97.8 %all-to-all-start.3 = ((bf16[8,192,4096]{2,1,0:T(8,128)(2,1)}), bf16[8,192,4096]{2,1,0:T(8,128)(2,1)}, u32[]{:S(2)}, u32[]{:S(2)}) async-start(bf16[8,192,4096]{2,1,0:T(8,128)(2,1)} %bitcast.67), calls=%async_computation.3 | async-start | bytes 25165824 | tf_op jit(solution)/shard_map/all_to_all | solution.py:117
  934.8 138.1 %all-to-all-done.3 = bf16[8,192,4096]{2,1,0:T(8,128)(2,1)} async-done(((bf16[8,192,4096]{2,1,0:T(8,128)(2,1)}), bf16[8,192,4096]{2,1,0:T(8,128)(2,1)}, u32[]{:S(2)}, u32[]{:S(2)}) %all-to-all-start.3) | async-done | bytes 12582944 | tf_op jit(solution)/shard_map/all_to_all | solution.py:117
  1072.8 14.8 gather_fusion.8
  1097.3 13.5 reduce_sum.104
  1115.1 1938.7 %all-reduce.8.cloned.1.call-done = (f32[1,4096,1376]{2,1,0:T(8,128)}, f32[1,4096,1376]{2,1,0:T(8,128)}, f32[1,1376,4096]{2,1,0:T(8,128)}) async-done(((f32[1,4096,1376]{2,1,0:T(8,128)}, f32[1,4096,1376]{2,1,0:T(8,128)}, f32[1,1376,4096]{2,1,0:T(8,128)}), (f32[1,4096,1376]{2,1,0:T(8,128)}, f32[1,4096,1376]{2,1,0:T(8,128)}, f32[1,1376,4096]{2,1,0:T(8,128)})) %all-reduce.8.cloned.1.call-update) | async-done | bytes 67633168 | tf_op jit(solution)/shard_map/psum | solution.py:113
  3053.8 23.0 copy.63
  3076.8 23.0 copy.64
  3099.9 86.3 %all-reduce.6.cloned.1.call-done = f32[4096,8]{0,1:T(8,128)} async-done(((f32[4096,8]{0,1:T(8,128)}), f32[4096,8]{0,1:T(8,128)}) %all-reduce.6.cloned.1.call-update) | async-done | bytes 131088 | tf_op jit(solution)/shard_map/psum | solution.py:125
  3186.1 16.2 copy.81
  (143 shorter events, 148.8 us)
Async XLA Ops:
  7.2 46.4 %copy-start = (bf16[256,4096]{1,0:T(8,128)(2,1)S(1)}, bf16[256,4096]{1,0:T(8,128)(2,1)}, u32[]{:S(2)}) copy-start(bf16[256,4096]{1,0:T(8,128)(2,1)} %param.9) | copy-start | bytes 6291460
  10.1 217.0 %copy-start.16 = (s32[8]{0:T(128)}, s32[8]{0:T(128)S(1)}, u32[]{:S(2)}) copy-start(s32[8]{0:T(128)S(1)} %get-tuple-element.69) | copy-start | bytes 100
  220.4 5.5 copy-start.19
  220.4 237.8 %all-to-all-start.2 = ((bf16[8,192,4096]{2,1,0:T(8,128)(2,1)}), bf16[8,192,4096]{2,1,0:T(8,128)(2,1)}, u32[]{:S(2)}, u32[]{:S(2)}) async-start(bf16[8,192,4096]{2,1,0:T(8,128)(2,1)} %get-tuple-element.85), calls=%async_computation.2 | async-start | bytes 25165824 | tf_op jit(solution)/shard_map/all_to_all | solution.py:95
  399.2 13.4 copy-start.10
  399.2 14.0 copy-start.5
  429.7 124.2 %copy-start.8 = (s32[2048]{0:T(1024)}, s32[2048]{0:T(1024)S(1)}, u32[]{:S(2)}) copy-start(s32[2048]{0:T(1024)S(1)} %pad_clamp_fusion) | copy-start | bytes 24580
  541.3 63.4 %copy-start.15 = (s32[512,1]{0,1:T(1,128)S(1)}, s32[512,1]{0,1:T(1,128)}, u32[]{:S(2)}) copy-start(s32[512,1]{0,1:T(1,128)} %get-tuple-element.80) | copy-start | bytes 6148
  541.3 72.3 %copy-start.12 = (s32[2048]{0:T(1024)S(1)}, s32[2048]{0:T(1024)}, u32[]{:S(2)}) copy-start(s32[2048]{0:T(1024)} %get-tuple-element.113) | copy-start | bytes 24580
  553.9 69.3 %copy-start.17 = (s32[8]{0:T(128)S(1)}, s32[8]{0:T(128)}, u32[]{:S(2)}) copy-start(s32[8]{0:T(128)} %copy-done.16) | copy-start | bytes 100
  563.0 46.2 %all-to-all-start.4 = ((f32[8,192,1]{1,2,0:T(1,128)}), f32[8,192,1]{1,2,0:T(1,128)S(1)}, u32[]{:S(2)}, u32[]{:S(2)}) async-start(f32[8,192,1]{1,2,0:T(1,128)} %all_to_all.46), calls=%async_computation.4 | async-start | bytes 16384 | tf_op jit(solution)/shard_map/all_to_all | solution.py:118
  604.7 4.6 copy-start.13
  612.6 0.8 copy-start.1
  613.4 29.0 copy-start.3
  623.8 19.8 all-to-all-start
  627.2 2426.6 %all-reduce.8.cloned.1.call-start = ((), (), s32[]{:S(2)}) async-start(), calls=%async_computation.6 | async-start | bytes 137363456 | tf_op jit(solution)/shard_map/psum | solution.py:113
  785.9 21.2 copy-start.9
  835.3 98.1 %copy-start.2 = (f32[256,2]{1,0:T(8,128)S(1)}, f32[256,2]{1,0:T(8,128)}, u32[]{:S(2)}) copy-start(f32[256,2]{1,0:T(8,128)} %copy-done.1) | copy-start | bytes 6148
  835.3 98.1 %copy-start.4 = (f32[256,2]{1,0:T(8,128)S(1)}, f32[256,2]{1,0:T(8,128)}, u32[]{:S(2)}) copy-start(f32[256,2]{1,0:T(8,128)} %copy-done.3) | copy-start | bytes 6148
  835.3 98.1 %copy-start.18 = (f32[256]{0:T(256)S(1)}, f32[256]{0:T(256)}, u32[]{:S(2)}) copy-start(f32[256]{0:T(256)} %get-tuple-element.73) | copy-start | bytes 3076
  835.3 98.3 %copy-start.11 = (s32[256,2]{0,1:T(2,128)S(1)}, s32[256,2]{0,1:T(2,128)}, u32[]{:S(2)}) copy-start(s32[256,2]{0,1:T(2,128)} %param.10) | copy-start | bytes 6148
  835.4 237.5 %copy-start.14 = (s32[1024]{0:T(1024)S(1)}, s32[1024]{0:T(1024)}, u32[]{:S(2)}) copy-start(s32[1024]{0:T(1024)} %copy-done.13) | copy-start | bytes 12292
  835.4 237.5 %all-to-all-start.3 = ((bf16[8,192,4096]{2,1,0:T(8,128)(2,1)}), bf16[8,192,4096]{2,1,0:T(8,128)(2,1)}, u32[]{:S(2)}, u32[]{:S(2)}) async-start(bf16[8,192,4096]{2,1,0:T(8,128)(2,1)} %bitcast.67), calls=%async_computation.3 | async-start | bytes 25165824 | tf_op jit(solution)/shard_map/all_to_all | solution.py:117
  933.2 2252.9 %all-reduce.6.cloned.1.call-start = ((), (), s32[]{:S(2)}) async-start(), calls=%async_computation.5 | async-start | bytes 262144 | tf_op jit(solution)/shard_map/psum | solution.py:125
  1087.6 23.2 copy-start.6
  3186.1 16.2 copy-start.7
Sparse Core Ops, SparseCore 0:
  755.6 2298.1 all-reduce.7
  3059.9 126.1 all-reduce.5
where the time goes:
time: 3220 us; the launch traced here: 3210 us
  waiting for transfers between devices  2170 us (67%)
  local copies, waits for them, and re-layouts  316 us (10%)
  blocking collectives  284 us (9%)
  Pallas kernels  157 us (5%)
  starting transfers between devices  149 us (5%)
  other arithmetic  116 us (4%)
    psum x1, waiting for transfers between devices, device_step(): grad_gate = lax.psum(grad_gate, 'dp')  1940 us
    all_to_all x1, blocking collectives, device_step(): dy_recv = lax.all_to_all(dy_send, 'ep', 0, 0, tiled=True)  144 us
    unnamed x1, blocking collectives  140 us
    all_to_all x1, waiting for transfers between devices, device_step(): dx_back = lax.all_to_all(dx_rows[return_pos], 'ep', 0, 0, tiled=True)  138 us
    unnamed x51, local copies, waits for them, and re-layouts  110 us
    another operation x6, Pallas kernels  109 us
    all_to_all x1, starting transfers between devices, device_step(): dx_back = lax.all_to_all(dx_rows[return_pos], 'ep', 0, 0, tiled=True)  97.8 us
    psum x1, waiting for transfers between devices, device_step(): grad_router = lax.psum(grad_router, ('dp', 'ep'))  86.3 us
  transfers between devices with their start and end apart: 6, of which 4 were waited for; matrix products, arithmetic and copies ran while one was open for 8% of the time, Pallas kernels for 1%

commit v1 on v0

v1 whole, which is shorter than its diff:
```python
import functools

import jax
import jax.numpy as jnp
from jax import lax
from jax.experimental import pallas as pl
from jax.experimental.pallas import tpu as pltpu
from jax.sharding import PartitionSpec as P

BF = jnp.bfloat16
F32 = jnp.float32
MESH = pl.DeviceIdType.MESH
ANY = pl.BlockSpec(memory_space=pl.ANY)
NT = (((1,), (1,)), ((), ()))
TN = (((0,), (0,)), ((), ()))
NN = (((1,), (0,)), ((), ()))
VMEM_LIMIT = 67_000_000
NOWHERE = 300.0


def mm(left, right, dims=NN):
    return lax.dot_general(left, right, dims, preferred_element_type=F32)


def where_am_i():
    z = lax.axis_index("dp")
    e = lax.axis_index("ep")
    return z, e, e // 4, (e // 2) % 2, e % 2


def shard_of(z, y, x, c):
    return z * 8 + y * 4 + x * 2 + c


def other_levels(z):
    return z + 1 - 2 * (z % 2), 2 - z // 2, 3 - 3 * (z // 2)


class Shapes:
    def __init__(self, tokens, width, hidden, cap):
        self.t, self.d, self.f, self.cap = tokens, width, hidden, cap
        self.pair = 2 * cap
        self.wide = min(512, width)
        half = (hidden // 2 + 127) // 128 * 128
        self.cuts = [(0, half), (half, hidden)] if half < hidden else [(0, hidden)]


class Links:
    def __init__(self, bufs, own, ssem, rsem, partner):
        self.bufs, self.own, self.ssem, self.rsem, self.partner = bufs, own, ssem, rsem, partner
        self.sent = {}

    def _copy(self, slot, part, sid, dev, own):
        src = self.own[part] if own else self.bufs[part].at[sid]
        return pltpu.make_async_remote_copy(
            src_ref=src,
            dst_ref=self.bufs[part].at[sid],
            send_sem=self.ssem.at[slot, part],
            recv_sem=self.rsem.at[sid, part],
            device_id=dev,
            device_id_type=MESH,
        )

    def _do(self, when, go):
        if when is None:
            go()
        else:
            pl.when(when())(go)

    def send(self, tag, sid, dev, parts=(0, 1, 2), when=None, own=False):
        if tag not in self.sent:
            self.sent[tag] = (len(self.sent), sid, dev, parts, when, own)
        slot = self.sent[tag][0]

        def go():
            for part in parts:
                self._copy(slot, part, sid(), dev, own).start()

        self._do(when, go)

    def arrived(self, sid, parts=(0, 1, 2), when=None):
        def go():
            for part in parts:
                self._copy(0, part, sid(), self.partner, False).wait_recv()

        self._do(when, go)

    def drain(self):
        for slot, sid, dev, parts, when, own in self.sent.values():

            def go():
                for part in parts:
                    self._copy(slot, part, sid(), dev, own).wait_send()

            self._do(when, go)

    def along_column(self, name, step, z, shard, above, below):
        top, bottom = (lambda: shard(z + step)), (lambda: shard(z - step))
        has_top, has_bottom = (lambda: z + step <= 3), (lambda: z >= step)
        self.arrived(top, when=has_top)
        if step < 3:
            self.send((name, step, 0), top, below, when=lambda: jnp.logical_and(has_top(), z > 0))
        self.send((name, step, 1), top, self.partner, when=has_top)
        self.arrived(bottom, when=has_bottom)
        if step < 3:
            self.send((name, step, 2), bottom, above, when=lambda: jnp.logical_and(has_bottom(), z < 3))
        self.send((name, step, 3), bottom, self.partner, when=has_bottom)


def enter(z, peers, above, below):
    barrier = pltpu.get_barrier_semaphore()

    def greet(dev):
        pl.semaphore_signal(barrier, inc=1, device_id=dev, device_id_type=MESH)

    for dev in peers:
        greet(dev)

    @pl.when(z < 3)
    def _():
        greet(above)

    @pl.when(z > 0)
    def _():
        greet(below)

    pl.semaphore_wait(barrier, len(peers) + (5 - z) // 3 + (z + 2) // 3)


def load_weights(weights, w_vmem, w_sem):
    for k in range(3):
        pltpu.make_async_copy(weights[k], w_vmem.at[k], w_sem.at[k]).start()


def await_weights(weights, w_vmem, w_sem):
    for k in range(3):
        pltpu.make_async_copy(weights[k], w_vmem.at[k], w_sem.at[k]).wait()


def pick_rows(sh, half, stage, meta, expert, xs, do, gs):
    cap, t, wide = sh.cap, sh.t, sh.wide
    pos = meta[half, pl.ds(expert, 1), :]
    gate = meta[half, pl.ds(8 + expert, 1), :]
    slot = lax.broadcasted_iota(jnp.int32, (cap, t), 0).astype(F32)
    hit = slot == pos
    pick = jnp.where(hit, 1.0, 0.0).astype(BF)
    gate_col = jnp.sum(jnp.where(hit, gate, 0.0), axis=1, keepdims=True)
    rows = slice(half * cap, (half + 1) * cap)
    for n in range(0, sh.d, wide):
        cols = slice(n, n + wide)
        xs[rows, cols] = mm(pick, stage[2 * half, :, cols]).astype(BF)
        g_sel = mm(pick, stage[2 * half + 1, :, cols])
        do[rows, cols] = (gate_col * g_sel).astype(BF)
        if gs is not None:
            gs[rows, cols] = g_sel.astype(BF)


def expert_rows(sh, w, xs, do, a, d1, d3):
    for lo, hi in sh.cuts:
        cols = slice(lo, hi)
        z1 = mm(xs[...], w[0, cols, :], NT)
        z3 = mm(xs[...], w[1, cols, :], NT)
        da = mm(do[...], w[2, cols, :], NT)
        sig = jax.nn.sigmoid(z1)
        silu = z1 * sig
        a[:, cols] = (silu * z3).astype(BF)
        d1[:, cols] = (da * z3 * sig * (1.0 + z1 * (1.0 - sig))).astype(BF)
        d3[:, cols] = (da * silu).astype(BF)


def token_rows(sh, w, a, d1, d3, gs, q):
    acc = jnp.zeros((sh.pair, 1), F32)
    for n in range(0, sh.d, sh.wide):
        cols = slice(n, n + sh.wide)
        out = mm(a[...], w[2, :, cols])
        acc = acc + jnp.sum(out * gs[:, cols].astype(F32), axis=1, keepdims=True)
    q[...] = jnp.broadcast_to(acc, q.shape)
    for n in range(0, sh.d, sh.wide):
        cols = slice(n, n + sh.wide)
        row = mm(d1[...], w[0, :, cols]) + mm(d3[...], w[1, :, cols])
        gs[:, cols] = row.astype(BF)


class Rows:
    def __init__(self, sh, expert, bufs, own, w, vm, sems, hbm):
        self.sh, self.expert, self.bufs, self.own, self.w = sh, expert, bufs, own, w
        self.stage, self.meta, self.xs, self.do, self.a, self.d1, self.d3 = vm
        self.in_sem, self.out_sem = sems
        self.xs_h, self.do_h, self.d_h = hbm

    def _in(self, half, part, sid, own=False):
        src = self.own[part] if own else self.bufs[part].at[sid]
        dst = self.meta.at[half] if part == 2 else self.stage.at[2 * half + part]
        return pltpu.make_async_copy(src, dst, self.in_sem.at[half, part])

    def load(self, sids, own_first=None):
        for half in range(2):
            for part in (2, 0, 1):
                if half == 0 and own_first is not None:

                    @pl.when(own_first)
                    def _():
                        self._in(half, part, sids[half], True).start()

                    @pl.when(jnp.logical_not(own_first))
                    def _():
                        self._in(half, part, sids[half]).start()
                else:
                    self._in(half, part, sids[half]).start()

    def select(self, sids, gs=None):
        for half in range(2):
            for part in (2, 0, 1):
                self._in(half, part, sids[half]).wait()
            pick_rows(self.sh, half, self.stage, self.meta, self.expert, self.xs, self.do, gs)

    def _out(self, k, row0):
        at = pl.ds(row0, self.sh.pair)
        src = (self.xs, self.do, self.d1, self.d3, self.a)[k]
        dst = (self.xs_h, self.do_h)[k].at[at, :] if k < 2 else self.d_h.at[k - 2, at, :]
        return pltpu.make_async_copy(src, dst, self.out_sem.at[k])

    def forward(self, row0):
        for k in (0, 1):
            self._out(k, row0).start()
        expert_rows(self.sh, self.w, self.xs, self.do, self.a, self.d1, self.d3)
        for k in (2, 3, 4):
            self._out(k, row0).start()

    def finish(self, row0):
        for k in range(5):
            self._out(k, row0).wait()


def add_weight_grads(sh, rows, hbm, grad_in, put, vm, sems, tick=None):
    xs_h, do_h, d_h = hbm
    d_v, y_v, acc = vm
    d_sem, y_sem, i_sem, o_sem = sems
    nblk = sh.d // sh.wide
    total = 3 * nblk

    def d_copy(k):
        return pltpu.make_async_copy(d_h.at[k, pl.ds(0, rows), :], d_v.at[k % 2], d_sem.at[k % 2])

    def y_copy(it, slot, src):
        col = pl.multiple_of((it % nblk) * sh.wide, sh.wide)
        return pltpu.make_async_copy(src.at[pl.ds(0, rows), pl.ds(col, sh.wide)], y_v.at[slot], y_sem.at[slot])

    def y_start(it):
        @pl.when(it < 2 * nblk)
        def _():
            y_copy(it, it % 2, xs_h).start()

        @pl.when(it >= 2 * nblk)
        def _():
            y_copy(it, it % 2, do_h).start()

    def acc_in(it):
        col = pl.multiple_of((it % nblk) * sh.wide, sh.wide)
        return pltpu.make_async_copy(grad_in.at[it // nblk, :, pl.ds(col, sh.wide)], acc.at[it % 3], i_sem.at[it % 3])

    def acc_out(it, start):
        col = pl.multiple_of((it % nblk) * sh.wide, sh.wide)
        put(it // nblk, col, acc.at[it % 3], o_sem.at[it % 3], start)

    d_copy(0).start()
    y_start(0)
    if grad_in is not None:
        acc_in(0).start()

    def body(it, carry):
        k = it // nblk

        @pl.when(it % nblk == 0)
        def _():
            @pl.when(k < 2)
            def _():
                d_copy(k + 1).start()

            d_copy(k).wait()

        @pl.when(it + 1 < total)
        def _():
            y_start(it + 1)

        @pl.when(it >= 2)
        def _():
            acc_out(it - 2, False)

        if grad_in is not None:

            @pl.when(it + 1 < total)
            def _():
                acc_in(it + 1).start()

        if tick is not None:
            tick(it)
        y_copy(it, it % 2, xs_h).wait()
        if grad_in is not None:
            acc_in(it).wait()
            acc[it % 3] += mm(d_v[k % 2], y_v[it % 2], TN)
        else:
            acc[it % 3] = mm(d_v[k % 2], y_v[it % 2], TN)
        acc_out(it, True)
        return carry

    lax.fori_loop(0, total, body, None)
    acc_out(total - 2, False)
    acc_out(total - 1, False)


def put_stacked(grads):
    def put(k, col, src, sem, start):
        copy = pltpu.make_async_copy(src, grads.at[k, :, pl.ds(col, src.shape[-1])], sem)
        copy.start() if start else copy.wait()

    return put


def put_separate(grads):
    def put(k, col, src, sem, start):
        if start:
            for j in range(3):

                @pl.when(k == j)
                def _():
                    pltpu.make_async_copy(src, grads[j].at[:, pl.ds(col, src.shape[-1])], sem).start()
        else:
            pltpu.make_async_copy(src, grads[0].at[:, pl.ds(col, src.shape[-1])], sem).wait()

    return put


def row_scratch(sh):
    return (
        pltpu.VMEM((3, sh.f, sh.d), BF),
        pltpu.VMEM((4, sh.t, sh.d), BF),
        pltpu.VMEM((2, 16, sh.t), F32),
        pltpu.VMEM((sh.pair, sh.d), BF),
        pltpu.VMEM((sh.pair, sh.d), BF),
        pltpu.VMEM((sh.pair, sh.f), BF),
        pltpu.VMEM((sh.pair, sh.f), BF),
        pltpu.VMEM((sh.pair, sh.f), BF),
    )


def grad_scratch(sh, rows):
    return (
        pltpu.VMEM((2, rows, sh.f), BF),
        pltpu.VMEM((2, rows, sh.wide), BF),
        pltpu.VMEM((3, sh.f, sh.wide), F32),
    )


GRAD_SEMS = [pltpu.SemaphoreType.DMA((2,)), pltpu.SemaphoreType.DMA((2,)), pltpu.SemaphoreType.DMA((3,)), pltpu.SemaphoreType.DMA((3,))]
ROW_SEMS = [pltpu.SemaphoreType.DMA((3,)), pltpu.SemaphoreType.DMA((2, 3)), pltpu.SemaphoreType.DMA((5,))]


def first_kernel(sh, x_in, g_in, m_in, w1, w3, w2, xb, gb, mb, rback, qback, r_h, q_h, xs_h, do_h, d_h, grads,
                 ssem, rsem, ret_s, ret_r, w_sem, in_sem, out_sem, loc_sem, *grad_sems):
    z, e, y, x, c = where_am_i()
    me = shard_of(z, y, x, c)
    bufs, own, weights = (xb, gb, mb), (x_in, g_in, m_in), (w1, w3, w2)
    partner, xn, yn = (z, e + 1 - 2 * c), (z, e + 2 - 4 * x), (z, e + 4 - 8 * y)
    above, below = (z + 1, e), (z - 1, e)
    links = Links(bufs, own, ssem, rsem, partner)
    column = [(y, x), (y, 1 - x), (1 - y, x), (1 - y, 1 - x)]
    mine = [shard_of(z, yy, xx, c) for yy, xx in column]
    theirs = [shard_of(z, yy, xx, 1 - c) for yy, xx in column]
    plane = [(z, yy * 4 + xx * 2 + cc) for yy, xx in column for cc in (c, 1 - c)]

    enter(z, plane[1:], above, below)
    links.send("p", lambda: me, partner, own=True)
    links.send("x", lambda: me, xn, own=True)
    links.send("y", lambda: me, yn, own=True)
    links.send("u", lambda: me, above, when=lambda: z < 3, own=True)
    links.send("d", lambda: me, below, when=lambda: z > 0, own=True)

    def line(step):
        links.along_column("o", step, z, lambda lev: shard_of(lev, y, x, c), above, below)

    def ret(k):
        for part, (src, dst) in enumerate(((r_h, rback), (q_h, qback))):
            yield pltpu.make_async_remote_copy(
                src_ref=src.at[k], dst_ref=dst.at[e], send_sem=ret_s.at[k, part], recv_sem=ret_r.at[e, part],
                device_id=plane[k], device_id_type=MESH)

    def ret_in(k):
        peer = plane[k][1]
        for part, (src, dst) in enumerate(((r_h, rback), (q_h, qback))):
            yield pltpu.make_async_remote_copy(
                src_ref=src.at[k], dst_ref=dst.at[peer], send_sem=ret_s.at[k, part], recv_sem=ret_r.at[peer, part],
                device_id=plane[k], device_id_type=MESH)

    def rows_phase(w, stage, meta, xs, do, a, d1, d3, gs, q, qt):
        load_weights(weights, w, w_sem)
        rows = Rows(sh, e, bufs, own, w, (stage, meta, xs, do, a, d1, d3), (in_sem, out_sem), (xs_h, do_h, d_h))

        def body(p, carry):
            @pl.when(p == 0)
            def _():
                links.arrived(lambda: theirs[0])

            @pl.when(p == 1)
            def _():
                links.arrived(lambda: mine[1])
                links.send("xy", lambda: mine[1], yn, parts=(1,))
                links.send("xp", lambda: mine[1], partner)
                links.arrived(lambda: mine[2])
                links.send("yx", lambda: mine[2], xn, parts=(0, 2))
                links.send("yp", lambda: mine[2], partner)
                line(1)
                links.arrived(lambda: theirs[1])

            @pl.when(p == 2)
            def _():
                links.arrived(lambda: theirs[2])

            @pl.when(p == 3)
            def _():
                links.arrived(lambda: mine[3])
                links.send("dp", lambda: mine[3], partner)
                links.arrived(lambda: theirs[3])

            yy = y + p // 2 - 2 * y * (p // 2)
            xx = x + p % 2 - 2 * x * (p % 2)
            sids = (shard_of(z, yy, xx, c), shard_of(z, yy, xx, 1 - c))
            row0 = pl.multiple_of(p * sh.pair, sh.pair)
            rows.load(sids, own_first=p == 0)
            rows.select(sids, gs)

            @pl.when(p == 0)
            def _():
                await_weights(weights, w, w_sem)

            rows.forward(row0)
            token_rows(sh, w, a, d1, d3, gs, q)
            qt[...] = jnp.transpose(q[...])[0:8, :]
            for half in range(2):
                at = slice(half * sh.cap, (half + 1) * sh.cap)

                @pl.when(p * 2 + half == 0)
                def _():
                    pltpu.make_async_copy(gs.at[at, :], rback.at[e], loc_sem.at[half]).start()
                    pltpu.make_async_copy(qt, qback.at[e], loc_sem.at[2 + half]).start()

                @pl.when(p * 2 + half > 0)
                def _():
                    pltpu.make_async_copy(gs.at[at, :], r_h.at[p * 2 + half], loc_sem.at[half]).start()
                    pltpu.make_async_copy(qt, q_h.at[p * 2 + half], loc_sem.at[2 + half]).start()

            for half in range(2):
                at = slice(half * sh.cap, (half + 1) * sh.cap)
                pltpu.make_async_copy(gs.at[at, :], r_h.at[p * 2 + half], loc_sem.at[half]).wait()
                pltpu.make_async_copy(qt, q_h.at[p * 2 + half], loc_sem.at[2 + half]).wait()
            for k in range(1, 8):

                @pl.when(p == k // 2)
                def _():
                    for copy in ret(k):
                        copy.start()

            rows.finish(row0)
            return carry

        lax.fori_loop(0, 4, body, None)

    pl.run_scoped(rows_phase, *row_scratch(sh), pltpu.VMEM((sh.pair, sh.d), BF), pltpu.VMEM((sh.pair, 128), F32),
                  pltpu.VMEM((8, sh.pair), F32))

    def tick(it):
        @pl.when(it == 1)
        def _():
            line(2)

    def grads_phase(*vm):
        add_weight_grads(sh, 4 * sh.pair, (xs_h, do_h, d_h), None, put_stacked(grads), vm, grad_sems, tick)

    pl.run_scoped(grads_phase, *grad_scratch(sh, 4 * sh.pair))
    line(3)
    for step in (1, 2, 3):
        links.arrived(lambda: shard_of(z + step, y, x, 1 - c), when=lambda: z + step <= 3)
        links.arrived(lambda: shard_of(z - step, y, x, 1 - c), when=lambda: z >= step)
    for k in range(1, 8):
        for copy in ret(k):
            copy.wait_send()
        for copy in ret_in(k):
            copy.wait_recv()
    links.drain()


def second_kernel(sh, xb_in, gb_in, mb_in, grads_in, w1, w3, w2, xb, gb, mb, grads, xs_h, do_h, d_h,
                  ssem, rsem, w_sem, in_sem, out_sem, *grad_sems):
    z, e, y, x, c = where_am_i()
    bufs, weights = (xb, gb, mb), (w1, w3, w2)
    partner, xn, yn = (z, e + 1 - 2 * c), (z, e + 2 - 4 * x), (z, e + 4 - 8 * y)
    above, below = (z + 1, e), (z - 1, e)
    links = Links(bufs, None, ssem, rsem, partner)
    levels = other_levels(z)
    f1, f2, f3 = levels

    enter(z, (partner, xn, yn), above, below)
    sides = ((y, 1 - x), (1 - y, x))

    def diag(lev):
        return shard_of(lev, 1 - y, 1 - x, c)

    links.send("u", lambda: diag(z), above, when=lambda: z < 3)
    links.send("d", lambda: diag(z), below, when=lambda: z > 0)
    for k in range(3):
        links.send(("x", k), lambda k=k: shard_of(levels[k], y, x, c), xn)
        links.send(("y", k), lambda k=k: shard_of(levels[k], y, x, c), yn)

    def stage(step):
        lev = levels[step - 1]
        for k, (yy, xx) in enumerate(sides):
            links.arrived(lambda: shard_of(lev, yy, xx, c))
            links.send(("p", step, k), lambda yy=yy, xx=xx: shard_of(lev, yy, xx, c), partner)
        links.along_column("d", step, z, diag, above, below)

    def theirs(step):
        lev = levels[step - 1]
        for yy, xx in sides:
            links.arrived(lambda: shard_of(lev, yy, xx, 1 - c))
        links.arrived(lambda: shard_of(z + step, 1 - y, 1 - x, 1 - c), when=lambda: z + step <= 3)
        links.arrived(lambda: shard_of(z - step, 1 - y, 1 - x, 1 - c), when=lambda: z >= step)

    hbm = (xs_h, do_h, d_h)
    blocks = 3 * (sh.d // sh.wide)

    def group(f, carry):
        def rows_phase(w, stage_v, meta, xs, do, a, d1, d3):
            load_weights(weights, w, w_sem)
            rows = Rows(sh, e, bufs, None, w, (stage_v, meta, xs, do, a, d1, d3), (in_sem, out_sem), hbm)

            def body(i, carry):
                first = (3 - f) // 3
                k = first * (i + 1) + (1 - first) * f
                lev = ((k - 2) * (k - 3) // 2) * f1 + ((k - 1) * (3 - k)) * f2 + ((k - 1) * (k - 2) // 2) * f3
                dx = (1 - first) * (1 - i % 2)
                dy = (1 - first) * ((i + 1) // 2)
                yy = y + dy - 2 * y * dy
                xx = x + dx - 2 * x * dx
                sids = (shard_of(lev, yy, xx, c), shard_of(lev, yy, xx, 1 - c))
                row0 = pl.multiple_of(i * sh.pair, sh.pair)
                rows.load(sids)
                rows.select(sids)

                @pl.when(i == 0)
                def _():
                    await_weights(weights, w, w_sem)

                rows.forward(row0)
                rows.finish(row0)
                return carry

            lax.fori_loop(0, 3, body, None)

        for step in (1, 2):

            @pl.when(f == step)
            def _():
                theirs(step)

        pl.run_scoped(rows_phase, *row_scratch(sh))

        def tick(it):
            @pl.when(jnp.logical_and(f == 0, it == blocks * 5 // 6))
            def _():
                stage(1)

            @pl.when(jnp.logical_and(f == 1, it == blocks // 2))
            def _():
                stage(2)

        def grads_phase(*vm):
            add_weight_grads(sh, 3 * sh.pair, hbm, grads, put_stacked(grads), vm, grad_sems, tick)

        pl.run_scoped(grads_phase, *grad_scratch(sh, 3 * sh.pair))
        return carry

    lax.fori_loop(0, 3, group, None)
    stage(3)
    theirs(3)
    links.drain()


def third_kernel(sh, xb, gb, mb, grads, w1, w3, w2, out1, out3, out2, xs_h, do_h, d_h, w_sem, in_sem, out_sem, *grad_sems):
    z, e, y, x, c = where_am_i()
    bufs, weights = (xb, gb, mb), (w1, w3, w2)
    lev = other_levels(z)[2]
    hbm = (xs_h, do_h, d_h)

    def rows_phase(w, stage_v, meta, xs, do, a, d1, d3):
        load_weights(weights, w, w_sem)
        rows = Rows(sh, e, bufs, None, w, (stage_v, meta, xs, do, a, d1, d3), (in_sem, out_sem), hbm)

        def body(i, carry):
            dx = 1 - i % 2
            dy = (i + 1) // 2
            yy = y + dy - 2 * y * dy
            xx = x + dx - 2 * x * dx
            sids = (shard_of(lev, yy, xx, c), shard_of(lev, yy, xx, 1 - c))
            row0 = pl.multiple_of(i * sh.pair, sh.pair)
            rows.load(sids)
            rows.select(sids)

            @pl.when(i == 0)
            def _():
                await_weights(weights, w, w_sem)

            rows.forward(row0)
            rows.finish(row0)
            return carry

        lax.fori_loop(0, 3, body, None)

    pl.run_scoped(rows_phase, *row_scratch(sh))

    def grads_phase(*vm):
        add_weight_grads(sh, 3 * sh.pair, hbm, grads, put_separate((out1, out3, out2)), vm, grad_sems)

    pl.run_scoped(grads_phase, *grad_scratch(sh, 3 * sh.pair))


def cost(sh, shards, products):
    return pl.CostEstimate(flops=2 * shards * sh.cap * sh.d * sh.f * products, bytes_accessed=300_000_000, transcendentals=0)


def solution(mesh):
    tok_spec = P(("dp", "ep"), None)
    exp_spec = P("ep", None, None)

    def device_step(x_loc, route_idx, w_router, w_gate, w_up, w_down, dy_loc):
        t, top_k = route_idx.shape
        d = x_loc.shape[1]
        n_exp = w_router.shape[1]
        f = w_down.shape[1]
        cap = 3 * t * top_k // n_exp
        sh = Shapes(t, d, f, cap)
        w1, w3, w2 = jnp.swapaxes(w_gate[0], 0, 1), jnp.swapaxes(w_up[0], 0, 1), w_down[0]

        logits = jnp.dot(x_loc, w_router, preferred_element_type=F32)
        experts = jnp.arange(n_exp, dtype=jnp.int32)
        chose = (route_idx[:, :, None] == experts).astype(F32)
        gate_probs = jax.nn.softmax(jnp.sum(chose * logits[:, None, :], axis=2), axis=-1)
        chose_any = jnp.sum(chose, axis=1)
        before = (jnp.arange(t)[:, None] > jnp.arange(t)[None, :]).astype(BF)
        rank = jnp.dot(before, chose_any.astype(BF), preferred_element_type=F32)
        pos = jnp.where(chose_any > 0, rank, NOWHERE)
        gate = jnp.sum(chose * gate_probs[:, :, None], axis=1)
        meta = jnp.concatenate([pos.T, gate.T], axis=0)
        slot = jnp.sum(chose * rank[:, None, :], axis=2).astype(jnp.int32)

        shape = jax.ShapeDtypeStruct
        gathered = [shape((32, t, d), BF), shape((32, t, d), BF), shape((32, 16, t), F32)]
        grads_shape = shape((3, f, d), F32)

        def row_shapes(pairs):
            n = pairs * sh.pair
            return [shape((n, d), BF), shape((n, d), BF), shape((3, n, f), BF)]

        outs = pl.pallas_call(
            functools.partial(first_kernel, sh),
            out_shape=gathered + [shape((n_exp, cap, d), BF), shape((n_exp, 8, sh.pair), F32), shape((8, cap, d), BF), shape((8, 8, sh.pair), F32)]
            + row_shapes(4) + [grads_shape],
            in_specs=[ANY] * 6,
            out_specs=[ANY] * 11,
            scratch_shapes=[pltpu.SemaphoreType.DMA((24, 3)), pltpu.SemaphoreType.DMA((32, 3)), pltpu.SemaphoreType.DMA((8, 2)), pltpu.SemaphoreType.DMA((8, 2))]
            + ROW_SEMS + [pltpu.SemaphoreType.DMA((4,))] + GRAD_SEMS,
            compiler_params=pltpu.CompilerParams(collective_id=0, has_side_effects=True, vmem_limit_bytes=VMEM_LIMIT),
            cost_estimate=cost(sh, 8, 9),
            name="own_level",
        )(x_loc, dy_loc, meta, w1, w3, w2)
        xb, gb, mb, rback, qback = outs[:5]
        grads = outs[-1]

        xb, gb, mb, grads = pl.pallas_call(
            functools.partial(second_kernel, sh),
            out_shape=gathered + [grads_shape] + row_shapes(3),
            in_specs=[ANY] * 7,
            out_specs=[ANY] * 7,
            input_output_aliases={0: 0, 1: 1, 2: 2, 3: 3},
            scratch_shapes=[pltpu.SemaphoreType.DMA((28, 3)), pltpu.SemaphoreType.DMA((32, 3))] + ROW_SEMS + GRAD_SEMS,
            compiler_params=pltpu.CompilerParams(collective_id=1, has_side_effects=True, vmem_limit_bytes=VMEM_LIMIT),
            cost_estimate=cost(sh, 18, 6),
            name="other_levels",
        )(xb, gb, mb, grads, w1, w3, w2)[:4]

        g1, g3, g2 = pl.pallas_call(
            functools.partial(third_kernel, sh),
            out_shape=[shape((f, d), F32)] * 3 + row_shapes(3),
            in_specs=[ANY] * 7,
            out_specs=[ANY] * 6,
            scratch_shapes=ROW_SEMS + GRAD_SEMS,
            compiler_params=pltpu.CompilerParams(vmem_limit_bytes=VMEM_LIMIT),
            cost_estimate=cost(sh, 6, 6),
            name="last_level",
        )(xb, gb, mb, grads, w1, w3, w2)[:3]

        at = route_idx * cap + slot
        dx_choice = rback.reshape(n_exp * cap, d)[at.reshape(-1)].reshape(t, top_k, d)
        q_half = qback[:, 0, :].reshape(n_exp, 2, cap)
        same = (experts % 2 == lax.axis_index("ep") % 2)[:, None]
        q_slot = jnp.where(same, q_half[:, 0], q_half[:, 1])
        hit = rank[:, :, None] == jnp.arange(cap, dtype=F32)
        q_tok = jnp.sum(jnp.where(hit, q_slot[None], 0.0), axis=2)
        dgate = jnp.sum(chose * q_tok[:, None, :], axis=2)
        d_sel = gate_probs * (dgate - jnp.sum(gate_probs * dgate, axis=1, keepdims=True))
        d_logits = jnp.sum(chose * d_sel[:, :, None], axis=1).astype(BF)
        du_router = lax.dot_general(d_logits, w_router, NT, preferred_element_type=F32)
        grad_router = lax.dot_general(x_loc, d_logits, TN, preferred_element_type=F32)
        grad_router = lax.psum(grad_router, ("dp", "ep"))
        grad_x = (jnp.sum(dx_choice.astype(F32), axis=1) + du_router).astype(BF)
        return grad_x, jnp.swapaxes(g1, 0, 1)[None], jnp.swapaxes(g3, 0, 1)[None], g2[None], grad_router

    return jax.shard_map(
        device_step, mesh=mesh, in_specs=(tok_spec, tok_spec, P(), exp_spec, exp_spec, exp_spec, tok_spec),
        out_specs=(tok_spec, exp_spec, exp_spec, exp_spec, P()), check_vma=False)
```

time: 3220 us -> 1020 us (0.32)
  waiting for transfers between devices: 2170 us -> 0.02 us
  Pallas kernels: 157 us -> 933 us
  local copies, waits for them, and re-layouts: 316 us -> 28 us
  blocking collectives: 284 us -> 0 us
  starting transfers between devices: 149 us -> 0.04 us
  other arithmetic: 116 us -> 16 us
    psum x1 -> x0, waiting for transfers between devices: 1940 us -> none  [device_step(): grad_gate = lax.psum(grad_gate, 'dp')]
    pallas_call x0 -> x3, Pallas kernels: none -> 933 us  [the longest x1 463 us: device_step(): pl.pallas_call(functools.partial(second_kernel, sh), out_shape=gathered +...]
    gather x23 -> x1, local copies, waits for them, and re-layouts: 191 us -> 14.8 us  [device_step(): rback.reshape(n_exp * cap, d)[at.reshape(-1)].reshape(t, top_k, d)]
    all_to_all x4 -> x0, starting transfers between devices: 148 us -> none  [the longest x1 97.8 us: device_step(): dx_back = lax.all_to_all(dx_rows[return_pos], 'ep', 0, 0, tiled=True)]
    all_to_all x1 -> x0, blocking collectives: 144 us -> none  [device_step(): dy_recv = lax.all_to_all(dy_send, 'ep', 0, 0, tiled=True)]
    all_to_all x4 -> x0, waiting for transfers between devices: 143 us -> none  [the longest x1 138 us: device_step(): dx_back = lax.all_to_all(dx_rows[return_pos], 'ep', 0, 0, tiled=True)]
    unnamed x1 -> x0, blocking collectives: 140 us -> none
    another operation x6 -> x0, Pallas kernels: 109 us -> none
  transfers between devices with their start and end apart: 6 -> 1, of which waited for: 4 -> 0; matrix products, arithmetic and copies ran while one was open for 8% -> 4% of each run, Pallas kernels for 1% -> 61%
where the time goes in v1:
time: 1020 us; the launch traced here: 1000 us
  Pallas kernels  933 us (91%)
  local copies, waits for them, and re-layouts  28 us (3%)
  other arithmetic  16 us (2%)
  between operations  14.6 us (1%)
    pallas_call x1, Pallas kernels, device_step(): pl.pallas_call(functools.partial(second_kernel, sh), out_shape=gathered +...  463 us
    pallas_call x1, Pallas kernels, device_step(): pl.pallas_call(functools.partial(first_kernel, sh), out_shape=gathered +...  324 us
    pallas_call x1, Pallas kernels, device_step(): pl.pallas_call(functools.partial(third_kernel, sh), out_shape=[shape((f,...  146 us
  transfers between devices with their start and end apart: 1, of which 0 were waited for; matrix products, arithmetic and copies ran while one was open for 4% of the time, Pallas kernels for 61%

profile of v1, /device:TPU:0, one launch (start us, length us, event | category | flops | bytes accessed | tf_op | source)
XLA Modules:
  0.0 1000.8 jit_solution(6989407560796139497)
XLA Ops:
  7.2 0.0 all-reduce.2.cloned.1.call-start
  7.2 2.2 fusion.10
  9.5 0.7 select_reduce_fusion.5
  10.2 0.0 copy-start.9
  10.3 0.7 convert_reduce_fusion
  11.0 0.0 copy-done.9
  11.0 0.2 fusion.1
  11.1 0.6 copy-done
  11.7 0.6 pad_maximum_fusion.m_in
  12.4 0.0 copy-done.2
  12.4 0.0 copy-done.7
  12.4 0.0 copy-start.3
  12.4 0.0 copy-start.8
  12.4 0.0 copy-start.10
  12.4 324.3 %own_level.1 = (bf16[32,256,4096]{2,1,0:T(8,128)(2,1)}, bf16[32,256,4096]{2,1,0:T(8,128)(2,1)}, f32[32,16,256]{2,1,0:T(8,128)}, bf16[8,192,4096]{2,1,0:T(8,128)(...) custom-call(bf16[256,4096]{1,0:T(8,128)(2,1)} %x_in.1, ...), custom_call_target="tpu_custom_call" | custom-call | flops 155826782208 | bytes 300000000 | tf_op jit(solution)/shard_map/own_level/pallas_call | solution.py:663
  336.8 0.9 slice_reduce_fusion
  337.7 0.1 reshape_squeeze.3
  337.8 0.1 fusion.2
  337.9 0.3 select_reduce_fusion
  338.3 0.0 copy-start.5
  338.3 2.6 convolution_bitcast_fusion
  340.9 0.0 all-reduce.2.cloned.1.call-update
  341.0 0.1 copy.27
  341.1 0.1 reshape.166
  341.3 14.8 %gather_fusion = bf16[512,4096]{1,0:T(8,128)(2,1)} fusion(bf16[1536,4096]{1,0:T(8,128)(2,1)} %bitcast.33, s32[1024]{0:T(1024)S(1)} %pad_clamp_fusion), kind=kCustom, calls=%fused_computation | custom fusion | bytes 8390656 | tf_op jit(solution)/shard_map/gather | solution.py:702
  356.1 9.6 reshape.167
  365.7 13.5 %reduce_sum.95 = f32[256,4096]{1,0:T(8,128)} reduce(f32[256,2,4096]{2,1,0:T(2,128)} %reshape.167, f32[]{:T(128)} %constant.35.clone.1), dimensions={1}, to_apply=%region_6.7 | reduce | flops 1048576 | bytes 12582916 | tf_op jit(solution)/shard_map/reduce_sum | solution.py:714
  379.2 462.9 %other_levels.1 = (bf16[32,256,4096]{2,1,0:T(8,128)(2,1)}, bf16[32,256,4096]{2,1,0:T(8,128)(2,1)}, f32[32,16,256]{2,1,0:T(8,128)}, f32[3,1376,4096]{2,1,0:T(8,12...) custom-call(bf16[32,256,4096]{2,1,0:T(8,128)(2,1)} %get-tuple-elemen, ...), custom_call_target="tpu_custom_call", output_to_operand_aliasing={{0}: (0, {}), {1}: (1, {}), {2}: (2, {}), {3}: (3, {})} | custom-call | flops 233740173312 | bytes 300000000 | tf_op jit(solution)/shard_map/other_levels/pallas_call | solution.py:678
  842.1 0.0 copy-start.6
  842.1 145.6 %last_level.1 = (f32[1376,4096]{1,0:T(8,128)}, f32[1376,4096]{1,0:T(8,128)}, f32[1376,4096]{1,0:T(8,128)}, bf16[1152,4096]{1,0:T(8,128)(2,1)}, bf16[1152,4096]{1...) custom-call(bf16[32,256,4096]{2,1,0:T(8,128)(2,1)} %get-tuple-element.24.xb, bf16[32,256,4096]{2,1,0:T(8,128)(2,1)} %get-tuple-element.25.gb, ...), custom_call_target="tpu_custom_call" | custom-call | flops 77913391104 | bytes 300000000 | tf_op jit(solution)/shard_map/last_level/pallas_call | solution.py:690
  987.8 4.3 fusion
  992.1 1.6 copy.40
  (26 shorter events, 0.2 us)
Async XLA Ops:
  7.2 984.9 %all-reduce.2.cloned.1.call-start = ((), (), s32[]{:S(2)}) async-start(), calls=%async_computation | async-start | bytes 262144 | tf_op jit(solution)/shard_map/psum | solution.py:713
  10.2 2.2 copy-start.2
  10.2 2.2 copy-start.7
  10.2 0.7 copy-start.9
  11.1 0.6 copy-start
  12.4 325.5 %copy-start.1 = (f32[256,8]{0,1:T(8,128)S(1)}, f32[256,8]{0,1:T(8,128)}, u32[]{:S(2)}) copy-start(f32[256,8]{0,1:T(8,128)} %copy-done) | copy-start | bytes 24580
  12.4 325.8 %copy-start.4 = (s32[256,2]{0,1:T(2,128)S(1)}, s32[256,2]{0,1:T(2,128)}, u32[]{:S(2)}) copy-start(s32[256,2]{0,1:T(2,128)} %param.8) | copy-start | bytes 6148
  12.4 325.8 %copy-start.3 = (f32[256,2]{0,1:T(2,128)S(1)}, f32[256,2]{0,1:T(2,128)}, u32[]{:S(2)}) copy-start(f32[256,2]{0,1:T(2,128)} %copy-done.2) | copy-start | bytes 6148
  12.4 325.8 %copy-start.8 = (f32[256]{0:T(256)S(1)}, f32[256]{0:T(256)}, u32[]{:S(2)}) copy-start(f32[256]{0:T(256)} %copy-done.7) | copy-start | bytes 3076
  12.4 325.8 %copy-start.10 = (f32[256]{0:T(256)S(1)}, f32[256]{0:T(256)}, u32[]{:S(2)}) copy-start(f32[256]{0:T(256)} %copy-done.9) | copy-start | bytes 3076
  338.3 17.8 %copy-start.5 = (bf16[256,8]{0,1:T(8,128)(2,1)}, bf16[256,8]{0,1:T(8,128)(2,1)S(1)}, u32[]{:S(2)}) copy-start(bf16[256,8]{0,1:T(8,128)(2,1)S(1)} %get-tuple-element.31) | copy-start | bytes 12292
  842.1 145.6 %copy-start.6 = (bf16[256,8]{0,1:T(8,128)(2,1)S(1)}, bf16[256,8]{0,1:T(8,128)(2,1)}, u32[]{:S(2)}) copy-start(bf16[256,8]{0,1:T(8,128)(2,1)} %copy-done.5) | copy-start | bytes 12292
Sparse Core Ops, SparseCore 0:
  341.1 127.2 all-reduce.1

commit v2 on v0

v2 whole, which is shorter than its diff:
```python
import functools

import jax
import jax.numpy as jnp
from jax import lax
from jax.experimental import pallas as pl
from jax.experimental.pallas import tpu as pltpu
from jax.sharding import PartitionSpec as P

BF = jnp.bfloat16
F32 = jnp.float32
MESH = pl.DeviceIdType.MESH
ANY = pl.BlockSpec(memory_space=pl.ANY)
NT = (((1,), (1,)), ((), ()))
TN = (((0,), (0,)), ((), ()))
NN = (((1,), (0,)), ((), ()))
TT = (((0,), (1,)), ((), ()))
VMEM_LIMIT = 67_000_000
NOWHERE = 300.0


def mm(left, right, dims=NN):
    return lax.dot_general(left, right, dims, preferred_element_type=F32)


def where_am_i():
    z = lax.axis_index("dp")
    e = lax.axis_index("ep")
    return z, e, e // 4, (e // 2) % 2, e % 2


def shard_of(z, y, x, c):
    return z * 8 + y * 4 + x * 2 + c


def other_levels(z):
    return z + 1 - 2 * (z % 2), 2 - z // 2, 3 - 3 * (z // 2)


class Shapes:
    def __init__(self, tokens, width, hidden, cap):
        self.t, self.d, self.f, self.cap = tokens, width, hidden, cap
        self.pair = 2 * cap
        self.wide = min(512, width)
        self.whole = hidden // 256 * 256
        self.tail = hidden - self.whole
        half = (self.whole // 2 + 255) // 256 * 256
        self.cuts = [(lo, hi) for lo, hi in ((0, half), (half, self.whole)) if lo < hi]


def rows_of(sh, half):
    return slice(half * sh.cap, (half + 1) * sh.cap)


class Links:
    def __init__(self, bufs, own, ssem, rsem, partner):
        self.bufs, self.own, self.ssem, self.rsem, self.partner = bufs, own, ssem, rsem, partner
        self.sent = {}

    def _copy(self, slot, part, sid, dev, own):
        src = self.own[part] if own else self.bufs[part].at[sid]
        return pltpu.make_async_remote_copy(
            src_ref=src,
            dst_ref=self.bufs[part].at[sid],
            send_sem=self.ssem.at[slot, part],
            recv_sem=self.rsem.at[sid, part],
            device_id=dev,
            device_id_type=MESH,
        )

    def _do(self, when, go):
        if when is None:
            go()
        else:
            pl.when(when())(go)

    def send(self, tag, sid, dev, parts=(0, 1, 2), when=None, own=False):
        if tag not in self.sent:
            self.sent[tag] = (len(self.sent), sid, dev, parts, when, own)
        slot = self.sent[tag][0]

        def go():
            for part in parts:
                self._copy(slot, part, sid(), dev, own).start()

        self._do(when, go)

    def arrived(self, sid, parts=(0, 1, 2), when=None):
        def go():
            for part in parts:
                self._copy(0, part, sid(), self.partner, False).wait_recv()

        self._do(when, go)

    def drain(self):
        for slot, sid, dev, parts, when, own in self.sent.values():

            def go():
                for part in parts:
                    self._copy(slot, part, sid(), dev, own).wait_send()

            self._do(when, go)

    def along_column(self, name, step, z, shard, above, below, where=None):
        ends = (lambda: z % 3 == 0)
        for side, sid, exists, onward, on_exists in (
            ("top", lambda: shard(z + step), lambda: z + step <= 3, below, lambda: z > 0),
            ("bottom", lambda: shard(z - step), lambda: z >= step, above, lambda: z < 3),
        ):

            def when(exists=exists):
                if where is None:
                    return exists()
                level = ends() if where == "ends" else jnp.logical_not(ends())
                return jnp.logical_and(exists(), level)

            self.arrived(sid, when=when)
            if step < 3 and where != "ends":
                self.send((name, step, side, where, "on"), sid, onward, when=lambda when=when, on=on_exists: jnp.logical_and(when(), on()))
            self.send((name, step, side, where, "partner"), sid, self.partner, when=when)


def enter(peers):
    barrier = pltpu.get_barrier_semaphore()
    for dev in peers:
        pl.semaphore_signal(barrier, device_id=dev, device_id_type=MESH)
    pl.semaphore_wait(barrier, len(peers))


def pick_rows(sh, half, stage, meta, expert, xs, do, gs):
    cap, t, wide = sh.cap, sh.t, sh.wide
    pos = meta[half, pl.ds(expert, 1), :]
    gate = meta[half, pl.ds(8 + expert, 1), :]
    slot = lax.broadcasted_iota(jnp.int32, (cap, t), 0).astype(F32)
    hit = slot == pos
    pick = jnp.where(hit, 1.0, 0.0).astype(BF)
    gate_col = jnp.sum(jnp.where(hit, gate, 0.0), axis=1, keepdims=True)
    rows = rows_of(sh, half)
    for n in range(0, sh.d, wide):
        cols = slice(n, n + wide)
        xs[rows, cols] = mm(pick, stage[2 * half, :, cols]).astype(BF)
        g_sel = mm(pick, stage[2 * half + 1, :, cols])
        do[rows, cols] = (gate_col * g_sel).astype(BF)
        gs[rows, cols] = g_sel.astype(BF)


def expert_rows(sh, w, w_tail, xs, do, a, d1, d3):
    def put(cols, z1, z3):
        da = mm(do[...], w[2, cols, :], NT)
        sig = jax.nn.sigmoid(z1)
        silu = z1 * sig
        a[:, cols] = (silu * z3).astype(BF)
        d1[:, cols] = (da * z3 * sig * (1.0 + z1 * (1.0 - sig))).astype(BF)
        d3[:, cols] = (da * silu).astype(BF)

    for lo, hi in sh.cuts:
        cols = slice(lo, hi)
        put(cols, mm(xs[...], w[0, cols, :], NT), mm(xs[...], w[1, cols, :], NT))
    both = mm(xs[...], w_tail[...], NT)
    put(slice(sh.whole, sh.f), both[:, : sh.tail], both[:, sh.tail :])


def token_rows(sh, w, a, d1, d3, gs, kept, qt):
    acc = jnp.zeros((sh.pair, 1), F32)
    for n in range(0, sh.d, sh.wide):
        cols = slice(n, n + sh.wide)
        out = mm(a[...], w[2, :, cols])
        acc = acc + jnp.sum(out * gs[:, cols].astype(F32), axis=1, keepdims=True)
    slot = lax.broadcasted_iota(jnp.int32, (sh.cap, sh.t), 0).astype(F32)
    for half in range(2):
        q = jnp.where(slot == kept[half, 0:1, :], acc[rows_of(sh, half), :], 0.0)
        qt[half] = jnp.broadcast_to(jnp.sum(q, axis=0, keepdims=True), (8, sh.t))
    for n in range(0, sh.d, sh.wide):
        cols = slice(n, n + sh.wide)
        row = mm(d1[...], w[0, :, cols]) + mm(d3[...], w[1, :, cols])
        gs[:, cols] = row.astype(BF)


class Rows:
    def __init__(self, sh, expert, bufs, own, w, vm, sems, hbm):
        self.sh, self.expert, self.bufs, self.own, self.w = sh, expert, bufs, own, w
        self.stage, self.meta, self.xs, self.do, self.a, self.d1, self.d3 = vm
        self.in_sem, self.out_sem = sems
        self.xs_h, self.do_h, self.d_h = hbm

    def _in(self, half, part, sid, own=False):
        src = self.own[part] if own else self.bufs[part].at[sid]
        dst = self.meta.at[half] if part == 2 else self.stage.at[2 * half + part]
        return pltpu.make_async_copy(src, dst, self.in_sem.at[half, part])

    def load(self, sids, own_first=False):
        for half in range(2):
            for part in (2, 0, 1):
                self._in(half, part, sids[half], own_first and half == 0).start()

    def select(self, sids, gs, kept):
        for half in range(2):
            for part in (2, 0, 1):
                self._in(half, part, sids[half]).wait()
            pick_rows(self.sh, half, self.stage, self.meta, self.expert, self.xs, self.do, gs)
            kept[half] = jnp.broadcast_to(self.meta[half, pl.ds(self.expert, 1), :], (8, self.sh.t))

    def out(self, k, row0):
        at = pl.ds(row0, self.sh.pair)
        src = (self.xs, self.do, self.d1, self.d3, self.a)[k]
        dst = (self.xs_h, self.do_h)[k].at[at, :] if k < 2 else self.d_h.at[k - 2, at, :]
        return pltpu.make_async_copy(src, dst, self.out_sem.at[k])

    def start_outs(self, row0, which):
        for k in which:
            self.out(k, row0).start()

    def wait_outs(self, row0, which):
        for k in which:
            self.out(k, row0).wait()


def add_weight_grads(sh, rows, hbm, grad_in, put, vm, sems, tick=None, fresh=None):
    xs_h, do_h, d_h = hbm
    d_v, y_v, acc = vm
    d_sem, y_sem, i_sem, o_sem = sems
    nblk = sh.d // sh.wide
    total = 3 * nblk
    ny, na = y_v.shape[0], acc.shape[0]

    def column(it):
        return pl.multiple_of((it % nblk) * sh.wide, sh.wide)

    def d_copy(k):
        return pltpu.make_async_copy(d_h.at[k, pl.ds(0, rows), :], d_v.at[k % 2], d_sem.at[k % 2])

    def y_copy(it, src):
        return pltpu.make_async_copy(src.at[pl.ds(0, rows), pl.ds(column(it), sh.wide)], y_v.at[it % ny], y_sem.at[it % ny])

    def acc_copy(it):
        return pltpu.make_async_copy(grad_in.at[it // nblk, :, pl.ds(column(it), sh.wide)], acc.at[it % na], i_sem.at[it % na])

    def acc_out(it, start):
        put(it // nblk, column(it), acc.at[it % na], o_sem.at[it % na], start)

    def fetch_y(it):
        @pl.when(it < 2 * nblk)
        def _():
            y_copy(it, xs_h).start()

        @pl.when(it >= 2 * nblk)
        def _():
            y_copy(it, do_h).start()

    def fetch_acc(it):
        if fresh is None:
            acc_copy(it).start()
        else:

            @pl.when(jnp.logical_not(fresh))
            def _():
                acc_copy(it).start()

    d_copy(0).start()
    fetch_y(0)
    fetch_acc(0)
    fetch_acc(1)

    def body(it, carry):
        k = it // nblk

        @pl.when(it % nblk == 0)
        def _():
            @pl.when(k < 2)
            def _():
                d_copy(k + 1).start()

            d_copy(k).wait()

        @pl.when(it >= 2)
        def _():
            acc_out(it - 2, False)

        @pl.when(it + 1 < total)
        def _():
            fetch_y(it + 1)

        @pl.when(it + 2 < total)
        def _():
            fetch_acc(it + 2)

        if tick is not None:
            tick(it)
        y_copy(it, xs_h).wait()

        def products(add):
            for lo in range(0, sh.f, sh.wide):
                at = slice(lo, min(lo + sh.wide, sh.f))
                new = mm(d_v[k % 2, :, at], y_v[it % ny], TN)
                acc[it % na, at, :] = acc[it % na, at, :] + new if add else new

        def add_products():
            acc_copy(it).wait()
            products(True)

        if fresh is None:
            add_products()
        else:
            pl.when(fresh)(lambda: products(False))
            pl.when(jnp.logical_not(fresh))(add_products)
        acc_out(it, True)
        return carry

    lax.fori_loop(0, total, body, None)
    acc_out(total - 2, False)
    acc_out(total - 1, False)


def put_stacked(grads):
    def put(k, col, src, sem, start):
        copy = pltpu.make_async_copy(src, grads.at[k, :, pl.ds(col, src.shape[-1])], sem)
        copy.start() if start else copy.wait()

    return put


def put_separate(grads):
    def put(k, col, src, sem, start):
        if start:
            for j in range(3):

                @pl.when(k == j)
                def _():
                    pltpu.make_async_copy(src, grads[j].at[:, pl.ds(col, src.shape[-1])], sem).start()
        else:
            pltpu.make_async_copy(src, grads[0].at[:, pl.ds(col, src.shape[-1])], sem).wait()

    return put


def row_scratch(sh):
    return (
        pltpu.VMEM((4, sh.t, sh.d), BF),
        pltpu.VMEM((2, 16, sh.t), F32),
        pltpu.VMEM((sh.pair, sh.d), BF),
        pltpu.VMEM((sh.pair, sh.d), BF),
        pltpu.VMEM((sh.pair, sh.f), BF),
        pltpu.VMEM((sh.pair, sh.f), BF),
        pltpu.VMEM((sh.pair, sh.f), BF),
    )


def grad_scratch(sh, rows):
    return (
        pltpu.VMEM((2, rows, sh.f), BF),
        pltpu.VMEM((2, rows, sh.wide), BF),
        pltpu.VMEM((4, sh.f, sh.wide), F32),
    )


GRAD_SEMS = [pltpu.SemaphoreType.DMA((2,)), pltpu.SemaphoreType.DMA((2,)), pltpu.SemaphoreType.DMA((4,)), pltpu.SemaphoreType.DMA((4,))]
ROW_SEMS = [pltpu.SemaphoreType.DMA((5,)), pltpu.SemaphoreType.DMA((2, 3)), pltpu.SemaphoreType.DMA((5,))]


def main_kernel(sh, x_in, g_in, m_in, w1, w3, w2, xb, gb, mb, rback, qback, r_h, q_h, xs_h, do_h, d_h, grads, router, w, w_tail,
                total, parts, q_v, m_v, ssem, rsem, ret_s, ret_r, sum_s, sum_r, sum_l, w_sem, in_sem, out_sem, loc_sem, *grad_sems):
    z, e, y, x, c = where_am_i()
    me = shard_of(z, y, x, c)
    bufs, own, weights = (xb, gb, mb), (x_in, g_in, m_in), (w1, w3, w2)
    partner, xn, yn = (z, e + 1 - 2 * c), (z, e + 2 - 4 * x), (z, e + 4 - 8 * y)
    above, below = (z + 1, e), (z - 1, e)
    links = Links(bufs, own, ssem, rsem, partner)
    levels = (z, *other_levels(z))
    columns = [(y, x), (y, 1 - x), (1 - y, x), (1 - y, 1 - x)]
    O, X, Y, D = range(4)
    places = " ".join(("O0 X0 Y0 O1", "D0 O2 X1 Y1", "D1 X2 Y2 O3", "D2 X3 Y3 D3")).split()
    order = [("OXYD".index(chip), int(level)) for chip, level in places]
    plane = [(z, yy * 4 + xx * 2 + cc) for yy, xx in columns for cc in (c, 1 - c)]

    def mine(col, k):
        return shard_of(levels[k], *columns[col], c)

    def theirs(col, k):
        return shard_of(levels[k], *columns[col], 1 - c)

    enter(plane[1:] + [((z + j) % 4, e) for j in (1, 2, 3)])
    links.send("p", lambda: me, partner, own=True)
    links.send("x", lambda: me, xn, own=True)
    links.send("y", lambda: me, yn, own=True)
    links.send("u", lambda: me, above, when=lambda: z < 3, own=True)
    links.send("d", lambda: me, below, when=lambda: z > 0, own=True)

    def column(name, step, where=None):
        col = O if name == "o" else D
        links.along_column(name, step, z, lambda lev: shard_of(lev, *columns[col], c), above, below, where)

    def sideways(k):
        links.send(("x", k), lambda: mine(O, k), xn)
        links.send(("y", k), lambda: mine(O, k), yn)

    def sides_in(k):
        for col in (X, Y):
            links.arrived(lambda: mine(col, k))
            links.send((col, k, "partner"), lambda col=col: mine(col, k), partner)

    def ret(k, part):
        src, dst = ((r_h, rback), (q_h, qback))[part]
        return pltpu.make_async_remote_copy(
            src_ref=src.at[k], dst_ref=dst.at[e], send_sem=ret_s.at[k, part], recv_sem=ret_r.at[e, part],
            device_id=plane[k], device_id_type=MESH)

    def ret_in(k, part):
        src, dst = ((r_h, rback), (q_h, qback))[part]
        peer = plane[k][1]
        return pltpu.make_async_remote_copy(
            src_ref=src.at[k], dst_ref=dst.at[peer], send_sem=ret_s.at[k, part], recv_sem=ret_r.at[peer, part],
            device_id=plane[k], device_id_type=MESH)

    def send_back(places, part=0):
        for k in places:
            ret(k, part).start()

    def hop(k):
        return pltpu.make_async_remote_copy(
            src_ref=total, dst_ref=parts.at[k], send_sem=sum_s.at[k], recv_sem=sum_r.at[k],
            device_id=(partner, xn, yn)[k], device_id_type=MESH)

    def level_hop(j):
        return pltpu.make_async_remote_copy(
            src_ref=total, dst_ref=parts.at[3 + z], send_sem=sum_s.at[2 + j], recv_sem=sum_r.at[3 + z],
            device_id=((z + j) % 4, e), device_id_type=MESH)

    def level_in(j):
        lev = (z + j) % 4
        return pltpu.make_async_remote_copy(
            src_ref=total, dst_ref=parts.at[3 + lev], send_sem=sum_s.at[2 + j], recv_sem=sum_r.at[3 + lev],
            device_id=(lev, e), device_id_type=MESH)

    def router_part(rows):
        for k in range(1, 8):
            ret_in(k, 1).wait_recv()
        x_rows = rows.at[0 : sh.t, :]
        copies = [pltpu.make_async_copy(src, dst, sum_l.at[k]) for k, (src, dst) in enumerate(((qback, q_v), (m_in, m_v), (x_in, x_rows)))]
        for copy in copies:
            copy.start()
        for copy in copies:
            copy.wait()
        gate, q = m_v[8:16, :], q_v[:, 0, :]
        d_sel = gate * (q - jnp.sum(gate * q, axis=0, keepdims=True))
        d_logits = d_sel.astype(BF)
        for n in range(0, sh.d, sh.wide):
            cols = slice(n, n + sh.wide)
            total[:, cols] = mm(d_logits, rows[0 : sh.t, cols])

    def add_hop(k):
        hop(k).wait()
        total[...] += parts[k]

    def before(n, rows):
        if n == 1:
            links.arrived(lambda: mine(X, 0))
            links.send("xy", lambda: mine(X, 0), yn, parts=(1,))
            links.arrived(lambda: mine(Y, 0))
            links.send("yx", lambda: mine(Y, 0), xn, parts=(0, 2))
            links.send("xp", lambda: mine(X, 0), partner)
            links.send("yp", lambda: mine(Y, 0), partner)
            column("o", 1)
            sideways(1)
        if n == 3:
            links.arrived(lambda: mine(D, 0))
            links.send("dp", lambda: mine(D, 0), partner)
            links.send("du", lambda: mine(D, 0), above, when=lambda: z < 3)
            links.send("dd", lambda: mine(D, 0), below, when=lambda: z > 0)
            send_back((1, 2, 3), part=1)
        if n == 4:
            send_back((4, 5), part=1)
        if n == 5:
            column("d", 1)
            router_part(rows)
            hop(0).start()
        if n == 6:
            add_hop(0)
            hop(1).start()
            send_back(range(1, 6))
        if n == 7:
            add_hop(1)
            hop(2).start()
        if n == 8:
            sides_in(2)
        if n == 9:
            column("o", 3)
            sideways(3)
        if n == 10:
            add_hop(2)
            for j in (1, 2, 3):
                level_hop(j).start()
            parts[3 + z] = total[...]
        if n == 12:
            column("d", 2, "ends")
        if n == 13:
            sides_in(3)
        if n == 15:
            column("d", 3)

    def during(g, it):
        if g == 0 and it == 1:
            send_back((6, 7), part=1)
            column("o", 2)
            sideways(2)
        if g == 0 and it == 12:
            sides_in(1)
        if g == 1 and it == 1:
            column("d", 2, "middle")
        if g == 1 and it == 4:
            send_back((6, 7))

    def pick(table, n):
        low, high = sum(v * 4**i for i, v in enumerate(table[:10])), sum(v * 4**i for i, v in enumerate(table[10:]))
        in_high = n // 10
        word = low * (1 - in_high) + high * in_high
        return lax.shift_right_logical(word, 2 * (n - 10 * in_high)) % 4

    def sids_of(n):
        col, k = pick([a for a, _ in order], n), pick([b for _, b in order], n)
        dx, dy = col % 2, col // 2
        yy, xx = y + dy - 2 * y * dy, x + dx - 2 * x * dx
        f1, f2, f3 = levels[1:]
        lev = (
            ((1 - k) * (2 - k) * (3 - k) // 6) * z
            + (k * (2 - k) * (3 - k) // 2) * f1
            + (k * (k - 1) * (3 - k) // 2) * f2
            + (k * (k - 1) * (k - 2) // 6) * f3
        )
        return shard_of(lev, yy, xx, c), shard_of(lev, yy, xx, 1 - c)

    ahead = (2, 3, 4, 6, 7, 8, 9, 11, 14)
    tail = pl.ds(sh.whole, sh.tail)
    weights_in = lambda: [pltpu.make_async_copy(weights[k], w.at[k], w_sem.at[k]) for k in range(3)] + [
        pltpu.make_async_copy(weights[k].at[tail, :], w_tail.at[pl.ds(k * sh.tail, sh.tail), :], w_sem.at[3 + k]) for k in range(2)
    ]
    for copy in weights_in():
        copy.start()
    blocks = 3 * (sh.d // sh.wide)

    def group(g, carry):
        def rows_phase(stage, meta, xs, do, a, d1, d3, gs, kept, qt):
            rows = Rows(sh, e, bufs, own, w, (stage, meta, xs, do, a, d1, d3), (in_sem, out_sem), (xs_h, do_h, d_h))

            def keep(n, start):
                for half in range(2):
                    at = rows_of(sh, half)
                    copies = lambda r, q: (
                        pltpu.make_async_copy(gs.at[at, :], r, loc_sem.at[half]),
                        pltpu.make_async_copy(qt.at[half], q, loc_sem.at[2 + half]),
                    )
                    place = n_place(n) * 2 + half
                    if not start:
                        for copy in copies(r_h.at[place], q_h.at[place]):
                            copy.wait()
                        continue


                    def go(r, q):
                        for copy in copies(r, q):
                            copy.start()

                    pl.when(place == 0)(lambda: go(rback.at[e], qback.at[e]))
                    pl.when(place > 0)(lambda: go(r_h.at[place], q_h.at[place]))

            def n_place(n):
                return n - n // 4

            def body(i, carry):
                pl.when(i < 5 + g // 2)(lambda: one_pair(i))
                return carry

            def one_pair(i):
                n = g * 5 + i
                sids, row0 = sids_of(n), pl.multiple_of(i * sh.pair, sh.pair)
                own_level = jnp.logical_and(n < 5, n != 3)
                for k in range(16):

                    @pl.when(n == k)
                    def _():
                        before(k, gs)
                        if k not in ahead:
                            links.arrived(lambda: theirs(*order[k]))
                            rows.load(sids, own_first=k == 0)

                @pl.when(i > 0)
                def _():
                    rows.wait_outs(row0, (0, 1))

                @pl.when(jnp.logical_and(n > 0, n < 4))
                def _():
                    keep(n - 1, False)

                rows.select(sids, gs, kept)
                rows.start_outs(row0, (0, 1))
                for k in ahead:

                    @pl.when(n + 1 == k)
                    def _():
                        links.arrived(lambda: theirs(*order[k]))
                        rows.load(sids_of(n + 1))

                @pl.when(n == 0)
                def _():
                    for copy in weights_in():
                        copy.wait()

                @pl.when(i > 0)
                def _():
                    rows.wait_outs(row0, (2, 3, 4))

                expert_rows(sh, w, w_tail, xs, do, a, d1, d3)
                rows.start_outs(row0, (2, 3, 4))

                @pl.when(own_level)
                def _():
                    token_rows(sh, w, a, d1, d3, gs, kept, qt)
                    keep(n, True)

                @pl.when(n == 4)
                def _():
                    keep(n, False)

            lax.fori_loop(0, 6, body, None)
            rows.wait_outs(0, range(5))

        pl.run_scoped(rows_phase, *row_scratch(sh), pltpu.VMEM((sh.pair, sh.d), BF), pltpu.VMEM((2, 8, sh.t), F32),
                      pltpu.VMEM((2, 8, sh.t), F32))

        def tick(it):
            for gg, when in ((0, 1), (0, 12), (1, 1), (1, 4)):

                @pl.when(jnp.logical_and(g == gg, it == when * blocks // 24))
                def _():
                    during(gg, when)

        @pl.when(g < 2)
        def _():
            def grads_phase(*vm):
                add_weight_grads(sh, 5 * sh.pair, (xs_h, do_h, d_h), grads, put_stacked(grads), vm, grad_sems, tick, g == 0)

            pl.run_scoped(grads_phase, *grad_scratch(sh, 5 * sh.pair))

        return carry

    lax.fori_loop(0, 3, group, None)
    for j in (1, 2, 3):
        level_hop(j).wait_send()
        level_in(j).wait_recv()
    total[...] = ((parts[3] + parts[4]) + parts[5]) + parts[6]
    copy = pltpu.make_async_copy(total, router, sum_l.at[0])
    copy.start()
    for k in range(1, 8):
        ret(k, 0).wait_send()
        ret(k, 1).wait_send()
        ret_in(k, 0).wait_recv()
    copy.wait()
    links.drain()


def last_kernel(sh, grads, xs_h, do_h, d_h, out1, out3, out2, *sems):
    def grads_phase(*vm):
        add_weight_grads(sh, 6 * sh.pair, (xs_h, do_h, d_h), grads, put_separate((out1, out3, out2)), vm, sems)

    pl.run_scoped(grads_phase, *grad_scratch(sh, 6 * sh.pair))


def cost(sh, shards, products):
    return pl.CostEstimate(flops=2 * shards * sh.cap * sh.d * sh.f * products, bytes_accessed=300_000_000, transcendentals=0)


def solution(mesh):
    tok_spec = P(("dp", "ep"), None)
    exp_spec = P("ep", None, None)

    def device_step(x_loc, route_idx, w_router, w_gate, w_up, w_down, dy_loc):
        t, top_k = route_idx.shape
        d = x_loc.shape[1]
        n_exp = w_router.shape[1]
        f = w_down.shape[1]
        cap = 3 * t * top_k // n_exp
        sh = Shapes(t, d, f, cap)
        w1, w3, w2 = jnp.swapaxes(w_gate[0], 0, 1), jnp.swapaxes(w_up[0], 0, 1), w_down[0]

        chosen = route_idx.T
        experts = jnp.arange(n_exp, dtype=jnp.int32)
        logits = mm(w_router, x_loc, TT)
        chose = (chosen[:, None, :] == experts[None, :, None]).astype(F32)
        gate_probs = jax.nn.softmax(jnp.sum(chose * logits[None], axis=1), axis=0)
        chose_any = jnp.sum(chose, axis=0)
        before = (jnp.arange(t)[:, None] < jnp.arange(t)[None, :]).astype(BF)
        rank = jnp.dot(chose_any.astype(BF), before, preferred_element_type=F32)
        pos = jnp.where(chose_any > 0, rank, NOWHERE)
        gate = jnp.sum(chose * gate_probs[:, None, :], axis=0)
        meta = jnp.concatenate([pos, gate], axis=0)

        shape = jax.ShapeDtypeStruct
        gathered = [shape((32, t, d), BF), shape((32, t, d), BF), shape((32, 16, t), F32)]
        n = 6 * sh.pair
        row_shapes = [shape((n, d), BF), shape((n, d), BF), shape((3, n, f), BF)]
        weights_vmem = pltpu.VMEM((3, f, d), BF)

        outs = pl.pallas_call(
            functools.partial(main_kernel, sh),
            out_shape=gathered + [shape((n_exp, cap, d), BF), shape((n_exp, 8, t), F32), shape((8, cap, d), BF), shape((8, 8, t), F32)]
            + row_shapes + [shape((3, f, d), F32), shape((n_exp, d), F32)],
            in_specs=[ANY] * 6,
            out_specs=[ANY] * 12,
            scratch_shapes=[weights_vmem, pltpu.VMEM((2 * sh.tail, d), BF), pltpu.VMEM((n_exp, d), F32), pltpu.VMEM((7, n_exp, d), F32), pltpu.VMEM((n_exp, 8, t), F32), pltpu.VMEM((16, t), F32), pltpu.SemaphoreType.DMA((48, 3)), pltpu.SemaphoreType.DMA((32, 3)), pltpu.SemaphoreType.DMA((8, 2)), pltpu.SemaphoreType.DMA((8, 2)),
                pltpu.SemaphoreType.DMA((6,)), pltpu.SemaphoreType.DMA((7,)), pltpu.SemaphoreType.DMA((3,))]
            + ROW_SEMS + [pltpu.SemaphoreType.DMA((4,))] + GRAD_SEMS,
            compiler_params=pltpu.CompilerParams(collective_id=0, has_side_effects=True, vmem_limit_bytes=VMEM_LIMIT),
            cost_estimate=cost(sh, 32, 5),
            name="gather_and_rows",
        )(x_loc, dy_loc, meta, w1, w3, w2)
        rback, qback, _, _, xs_h, do_h, d_h, grads, router = outs[3:]

        g1, g3, g2 = pl.pallas_call(
            functools.partial(last_kernel, sh),
            out_shape=[shape((f, d), F32)] * 3,
            in_specs=[ANY] * 4,
            out_specs=[ANY] * 3,
            scratch_shapes=GRAD_SEMS,
            compiler_params=pltpu.CompilerParams(vmem_limit_bytes=VMEM_LIMIT),
            cost_estimate=cost(sh, 12, 3),
            name="last_weight_grads",
        )(grads, xs_h, do_h, d_h)

        dgate = jnp.sum(chose * qback[None, :, 0, :], axis=1)
        d_sel = gate_probs * (dgate - jnp.sum(gate_probs * dgate, axis=0, keepdims=True))
        d_logits = jnp.sum(chose * d_sel[:, None, :], axis=0).astype(BF)
        du_router = mm(d_logits, w_router, TT)
        hit = (pos[:, None, :] == jnp.arange(cap, dtype=F32)[None, :, None]).astype(BF).reshape(n_exp * cap, t)
        rows_sum = mm(hit, rback.reshape(n_exp * cap, d), TN)
        grad_x = (rows_sum + du_router).astype(BF)
        return grad_x, jnp.swapaxes(g1, 0, 1)[None], jnp.swapaxes(g3, 0, 1)[None], g2[None], router.T

    return jax.shard_map(
        device_step, mesh=mesh, in_specs=(tok_spec, tok_spec, P(), exp_spec, exp_spec, exp_spec, tok_spec),
        out_specs=(tok_spec, exp_spec, exp_spec, exp_spec, P()), check_vma=False)
```

time: 3220 us -> 739 us (0.23)
  waiting for transfers between devices: 2170 us -> 0 us
  Pallas kernels: 157 us -> 720 us
  local copies, waits for them, and re-layouts: 316 us -> 4.14 us
  blocking collectives: 284 us -> 0 us
  starting transfers between devices: 149 us -> 0 us
  other arithmetic: 116 us -> 2.13 us
    psum x2 -> x0, waiting for transfers between devices: 2020 us -> none  [the longest x1 1940 us: device_step(): grad_gate = lax.psum(grad_gate, 'dp')]
    pallas_call x0 -> x2, Pallas kernels: none -> 720 us  [the longest x1 629 us: device_step(): pl.pallas_call(functools.partial(main_kernel, sh), out_shape=gathered + [...]
    gather x23 -> x0, local copies, waits for them, and re-layouts: 191 us -> none  [the longest x1 28.5 us: device_step(): x_recv[gather_pos]]
    all_to_all x4 -> x0, starting transfers between devices: 148 us -> none  [the longest x1 97.8 us: device_step(): dx_back = lax.all_to_all(dx_rows[return_pos], 'ep', 0, 0, tiled=True)]
    all_to_all x1 -> x0, blocking collectives: 144 us -> none  [device_step(): dy_recv = lax.all_to_all(dy_send, 'ep', 0, 0, tiled=True)]
    all_to_all x4 -> x0, waiting for transfers between devices: 143 us -> none  [the longest x1 138 us: device_step(): dx_back = lax.all_to_all(dx_rows[return_pos], 'ep', 0, 0, tiled=True)]
    unnamed x1 -> x0, blocking collectives: 140 us -> none
    another operation x6 -> x0, Pallas kernels: 109 us -> none
  transfers between devices with their start and end apart: 6 -> 0, of which waited for: 4 -> 0; matrix products, arithmetic and copies ran while one was open for 8% -> 0% of each run, Pallas kernels for 1% -> 0%
where the time goes in v2:
time: 739 us; the launch traced here: 738 us
  Pallas kernels  720 us (97%)
  matrix products  11 us (1%)
    pallas_call x1, Pallas kernels, device_step(): pl.pallas_call(functools.partial(main_kernel, sh), out_shape=gathered + [...  629 us
    pallas_call x1, Pallas kernels, device_step(): pl.pallas_call(functools.partial(last_kernel, sh), out_shape=[shape((f, d...  91.7 us

profile of v2, /device:TPU:0, one launch (start us, length us, event | category | flops | bytes accessed | tf_op | source)
XLA Modules:
  0.0 738.3 jit_solution(10303590817754220297)
XLA Ops:
  0.6 2.3 fusion.6
  2.9 0.7 select_reduce_fusion.3
  3.6 0.0 copy-start.1
  3.6 0.0 copy-start.4
  3.7 0.5 copy-done.1
  4.2 0.0 copy-start.6
  4.2 0.6 copy-done.6
  4.8 0.0 copy-done.4
  4.8 0.7 convert_reduce_fusion
  5.5 0.1 convolution_select_fusion
  5.6 0.0 copy-start.8
  5.6 0.6 copy-done.8
  6.2 0.6 pad_maximum_fusion.m_in
  6.8 0.0 copy-start.9
  6.8 628.6 %gather_and_rows.1 = (bf16[32,256,4096]{2,1,0:T(8,128)(2,1)}, bf16[32,256,4096]{2,1,0:T(8,128)(2,1)}, f32[32,16,256]{2,1,0:T(8,128)}, bf16[8,192,4096]{2,1,0:T(8...) custom-call(bf16[256,4096]{1,0:T(8,128)(2,1)} %x_in.1, ...), custom_call_target="tpu_custom_call" | custom-call | flops 346281738240 | bytes 300000000 | tf_op jit(solution)/shard_map/gather_and_rows/pallas_call | solution.py:702
  635.4 0.0 copy-done.9
  635.4 0.0 copy-start.3
  635.4 0.0 copy-start.2
  635.4 0.0 copy-start.5
  635.5 0.0 copy-start.7
  635.5 0.0 copy-start
  635.5 6.5 convolution_bitcast_fusion
  642.0 0.8 slice.3
  642.9 0.0 copy-done.3
  642.9 0.0 copy-done.2
  642.9 0.0 copy-done.5
  642.9 0.0 copy-done.7
  643.0 0.0 copy-done
  643.0 2.1 fusion
  645.1 91.7 %last_weight_grads.1 = (f32[1376,4096]{1,0:T(8,128)}, f32[1376,4096]{1,0:T(8,128)}, f32[1376,4096]{1,0:T(8,128)}) custom-call(f32[3,1376,4096]{2,1,0:T(8,128)} %get-tuple-element.17.grads, bf16[2304,4096]{1,0:T(8,128)(2,1)} %get-tuple-element.18.xs_h, bf16[2304,4096]{1,0:T(8,128)(2,1)} %get-tuple-element.19.do_h, bf16[3,2304,1376]{2,1,0:T(8,128)(2,1)} %get-tuple-element.20.d_h), custom_call_target="tpu_custom_call" | custom-call | flops 77913391104 | bytes 300000000 | tf_op jit(solution)/shard_map/last_weight_grads/pallas_call | solution.py:717
  736.8 1.6 copy.16
  (8 shorter events, 0.1 us)
Async XLA Ops:
  3.6 0.6 copy-start.1
  3.6 1.1 copy-start.4
  4.2 0.6 copy-start.6
  5.6 0.6 copy-start.8
  6.8 628.6 %copy-start.9 = (f32[8,256]{1,0:T(8,128)S(1)}, f32[8,256]{1,0:T(8,128)}, u32[]{:S(2)}) copy-start(f32[8,256]{1,0:T(8,128)} %copy-done.8) | copy-start | bytes 24580
  635.4 7.5 %copy-start.3 = (s32[256,2]{0,1:T(2,128)S(1)}, s32[256,2]{0,1:T(2,128)}, u32[]{:S(2)}) copy-start(s32[256,2]{0,1:T(2,128)} %param.8) | copy-start | bytes 6148
  635.4 7.5 %copy-start.2 = (f32[2,256]{1,0:T(2,128)S(1)}, f32[2,256]{1,0:T(2,128)}, u32[]{:S(2)}) copy-start(f32[2,256]{1,0:T(2,128)} %copy-done.1) | copy-start | bytes 6148
  635.4 7.5 %copy-start.5 = (f32[256]{0:T(256)S(1)}, f32[256]{0:T(256)}, u32[]{:S(2)}) copy-start(f32[256]{0:T(256)} %copy-done.4) | copy-start | bytes 3076
  635.5 7.5 %copy-start.7 = (f32[256]{0:T(256)S(1)}, f32[256]{0:T(256)}, u32[]{:S(2)}) copy-start(f32[256]{0:T(256)} %copy-done.6) | copy-start | bytes 3076
  635.5 7.5 %copy-start = (bf16[4096,8]{0,1:T(8,128)(2,1)S(1)}, bf16[4096,8]{0,1:T(8,128)(2,1)}, u32[]{:S(2)}) copy-start(bf16[4096,8]{0,1:T(8,128)(2,1)} %param.9) | copy-start | bytes 196612
